TPU v7x, 32 devices: a whole 2x2x4 slice. The times are simulated.
32 devices in a mesh: cls: 8 (over z, y), row: 4 (over x, core).
Axes of the slice: x: 2, y: 2, z: 4, core: 2. Of those that a mesh axis runs over, the one named last changes fastest.
Arguments:
- embeddings: float32 [1024, 1024], P('row'), may hold values from -6 to 6
- weights: float32 [1024, 81920], P(('cls', 'row')), may hold values from -4 to 4
- labels: int32 [1024], replicated, may hold values from 0 to 81919, as said below
Outputs:
- weight_update: float32 [1024, 81920], P(None, ('cls', 'row'))
- losses: float32 [2, 1024], replicated
Inputs may be any that keep to these rules, and one draw needn't show every extreme that they name: labels take at most 512 distinct values, at most one in each aligned run of 160 classes; rows may share a label.
All inputs are finite; a program needn't handle non-finite values.
Results may differ from a plain program's by a relative error of at most 0.012.
The roundings to bfloat16 on the way count: a program that leaves them out, or rounds other values in their place, can miss the bound.
Values may be sent and summed in bfloat16 or wider, within the bound.
No kernel may reach another device: no remote copies, remote signals or barrier semaphores. Data moves between devices by JAX's collectives and lax.ppermute only.
A program may use at most 128 MiB of HBM per device.

v0:
```python
import jax
import jax.numpy as jnp
from jax import lax
from jax.sharding import PartitionSpec as P

STEPS = 2
learn_rate = 2.0


def shards(embeddings, weights, labels):
    peer_count = lax.axis_size(("cls", "row"))
    examples = lax.all_gather(embeddings.astype(jnp.bfloat16), "row", axis=0, tiled=True)
    row_count = examples.shape[0]
    feature_rows = weights.shape[0]
    class_count = weights.shape[1] // peer_count
    model_width = feature_rows * peer_count
    offset = lax.axis_index(("cls", "row")) * class_count
    columns = lax.broadcasted_iota(jnp.int32, (1, class_count), 1) + offset
    label_hit = columns == labels[:, None]
    pieces = weights.reshape(feature_rows, peer_count, class_count // 128, 128)
    block_weights = lax.all_to_all(pieces, ("cls", "row"), split_axis=1, concat_axis=0, tiled=True)[
        :, 0
    ]
    block_width = block_weights.shape[1] * 128
    flat_weights = block_weights.reshape(block_weights.shape[0], block_width)
    block_logits = jnp.dot(
        examples, flat_weights.astype(jnp.bfloat16), preferred_element_type=jnp.float32
    )
    first_logits = block_logits.reshape(row_count, block_weights.shape[1], 128)
    current = block_weights.reshape(model_width, class_count)
    logits = first_logits.reshape(row_count, class_count)
    starting = current
    loss_rows = []
    for step_index in range(STEPS):
        if step_index > 0:
            logits = jnp.dot(
                examples, current.astype(jnp.bfloat16), preferred_element_type=jnp.float32
            )
        local_peak = jnp.max(logits, axis=1)
        local_picked = jnp.sum(jnp.where(label_hit, logits, 0.0), axis=1)
        row_peak = lax.pmax(local_peak, ("cls", "row"))
        row_total, picked = lax.psum(
            (jnp.sum(jnp.exp(logits - row_peak[:, None]), axis=1), local_picked), ("cls", "row")
        )
        log_norm = row_peak + jnp.log(row_total)
        loss_rows.append(log_norm - picked)
        onehot = jnp.where(label_hit, 1.0, 0.0)
        residual = (jnp.exp(logits - log_norm[:, None]) - onehot).astype(jnp.bfloat16)
        gradient = (
            lax.dot_general(
                examples, residual, (((0,), (0,)), ((), ())), preferred_element_type=jnp.float32
            )
            / row_count
        )
        current = current - learn_rate * gradient
    return (current - starting, jnp.stack(loss_rows))


def solution(mesh):
    placed = (P("row", None), P(("cls", "row"), None), P())
    return jax.shard_map(
        shards,
        mesh=mesh,
        in_specs=placed,
        out_specs=(P(None, ("cls", "row")), P()),
        check_vma=False,
    )
```

profile of v0, /device:TPU:0, one launch (start us, length us, event | category | flops | bytes accessed | tf_op | source)
XLA Modules:
  0.0 578.8 jit_solution(8699041707677321800)
XLA Ops:
  7.2 9.4 %reshape.18 = f32[32,32,20,128]{3,2,1,0:T(8,128)} reshape(f32[32,81920]{1,0:T(8,128)} %param.4) | data formatting | bytes 20971520 | tf_op jit(solution)/shard_map/reshape | solution.py:20
  16.6 14.7 %copy.13 = f32[32,32,20,128]{3,0,2,1:T(8,128)} copy(f32[32,32,20,128]{3,2,1,0:T(8,128)} %reshape.18) | data formatting | bytes 20971520 | tf_op jit(solution)/shard_map/reshape | solution.py:20
  31.3 0.0 copy-start
  31.3 7.4 %all-to-all-start = ((f32[32,32,20,128]{3,0,2,1:T(8,128)}), f32[32,32,20,128]{3,0,2,1:T(8,128)}, u32[]{:S(2)}, u32[]{:S(2)}) async-start(f32[32,32,20,128]{3,0,2,1:T(8,128)} %copy.13), calls=%async_computation | async-start | bytes 20971520 | tf_op jit(solution)/shard_map/all_to_all | solution.py:21
  38.8 0.4 all-gather.2.cloned.1.call-start
  39.2 0.0 copy-done
  39.2 0.9 convert_element_type.15
  40.1 0.0 all-gather.2.cloned.1.call-update
  40.1 234.6 %all-to-all-done = f32[32,32,20,128]{3,0,2,1:T(8,128)} async-done(((f32[32,32,20,128]{3,0,2,1:T(8,128)}), f32[32,32,20,128]{3,0,2,1:T(8,128)}, u32[]{:S(2)}, u32[]{:S(2)}) %all-to-all-start) | async-done | bytes 10485792 | tf_op jit(solution)/shard_map/all_to_all | solution.py:21
  274.7 17.8 %copy.14 = f32[32,32,1,20,128]{4,3,1,0,2:T(8,128)} copy(f32[32,32,1,20,128]{4,1,3,0,2:T(8,128)} %bitcast.1) | data formatting | bytes 20971520 | tf_op jit(solution)/shard_map/all_to_all | solution.py:21
  292.5 21.9 %copy.21 = f32[128,8,20,128]{3,1,2,0:T(8,128)} copy(f32[128,8,20,128]{3,2,1,0:T(8,128)} %bitcast.41) | data formatting | bytes 20971520
  314.4 11.4 %copy.15 = f32[1024,2560]{0,1:T(8,128)} copy(f32[1024,2560]{1,0:T(8,128)} %bitcast.42) | data formatting | bytes 20971520 | tf_op jit(solution)/shard_map/reshape;squeeze | solution.py:30
  325.8 0.0 copy-start.1
  325.8 11.4 %fusion.35 = (f32[1024]{0:T(1024)S(1)}, f32[1024,2560]{1,0:T(8,128)}) fusion(bf16[1024,1024]{1,0:T(8,128)(2,1)} %all-gather.2.cloned.1.call-done, f32[1024,2560]{1,0:T(8,128)} %bitcast.43), kind=kOutput, calls=%fused_computation.45 | convolution fusion | flops 5373950976 | bytes 23072768 | tf_op jit(solution)/shard_map/dot_general | solution.py:26
  337.2 36.8 %pmax.14 = f32[1024]{0:T(1024)S(1)} all-reduce(f32[1024]{0:T(1024)S(1)} %get-tuple-element.17), channel_id=1, replica_groups=mesh['cls'=8,'row'=4] {'cls','row'}, use_global_device_ids=true, to_apply=%region_1.2 | all-reduce | flops 1024 | bytes 8192 | tf_op jit(solution)/shard_map/pmax | solution.py:41
  374.0 0.0 copy-done.1
  374.0 5.7 fusion.4
  379.7 41.0 %psum.28 = f32[1024]{0:T(1024)S(1)} all-reduce(f32[1024]{0:T(1024)S(1)} %get-tuple-element.9), channel_id=1, replica_groups=mesh['cls'=8,'row'=4] {'cls','row'}, use_global_device_ids=true, to_apply=%region_3.4 | all-reduce | flops 1024 | bytes 8192 | tf_op jit(solution)/shard_map/psum | solution.py:42
  420.7 0.0 copy-start.2
  420.7 12.0 %fusion.14 = f32[2560,1024]{1,0:T(8,128)} fusion(bf16[1024,1024]{1,0:T(8,128)(2,1)} %all-gather.2.cloned.1.call-done, f32[1024,2560]{1,0:T(8,128)} %get-tuple-element.18, s32[2560]{0:T(1024)S(1)} %iota_add_fusion, f32[1024]{0:T(1024)S(1)} %log_add_fusion.1, s32[1024]{0:T(1024)S(1)} %copy-done.1), kind=kOutput, calls=%fused_computation.21 | convolution fusion | flops 5381816320 | bytes 23087104 | tf_op jit(solution)/shard_map/dot_general | solution.py:50
  432.8 0.0 slice-done
  432.8 0.0 slice-done.1
  432.8 0.0 slice-done.2
  432.8 0.0 copy-done.2
  432.8 12.4 %fusion.36 = (f32[1024]{0:T(1024)S(1)}, f32[2560,1024]{1,0:T(8,128)}) fusion(bf16[1024,1024]{1,0:T(8,128)(2,1)S(1)} %copy-done.2, f32[1024,2560]{0,1:T(8,128)S(1)} %bitcast.45, f32[2560,1024]{1,0:T(8,128)} %fusion.14), kind=kOutput, calls=%fused_computation.46 | convolution fusion | flops 5379193856 | bytes 33558528 | tf_op jit(solution)/shard_map/dot_general | solution.py:36
  445.2 39.6 %pmax.15 = f32[1024]{0:T(1024)S(1)} all-reduce(f32[1024]{0:T(1024)S(1)} %get-tuple-element.19), channel_id=1, replica_groups=mesh['cls'=8,'row'=4] {'cls','row'}, use_global_device_ids=true, to_apply=%region_5.6 | all-reduce | flops 1024 | bytes 8192 | tf_op jit(solution)/shard_map/pmax | solution.py:41
  484.8 11.5 %copy.16 = f32[2560,1024]{0,1:T(8,128)} copy(f32[2560,1024]{1,0:T(8,128)} %get-tuple-element.20) | data formatting | bytes 20971520 | tf_op jit(solution)/shard_map/dot_general | solution.py:36
  496.3 5.6 fusion.5
  501.9 40.6 %all-reduce = (f32[1024]{0:T(1024)S(1)}, f32[1024]{0:T(1024)S(1)}, f32[1024]{0:T(1024)S(1)}) all-reduce(f32[1024]{0:T(1024)S(1)} %get-tuple-element.11, f32[1024]{0:T(1024)S(1)} %get-tuple-element.10, f32[1024]{0:T(1024)S(1)} %get-tuple-element.8), channel_id=1, replica_groups=mesh['cls'=8,'row'=4] {'cls','row'}, use_global_device_ids=true, to_apply=%region_7.8 | all-reduce | flops 3072 | bytes 24576 | tf_op jit(solution)/shard_map/psum | solution.py:42
  542.5 17.2 %fusion.6 = f32[1024,2560]{0,1:T(8,128)} fusion(f32[1024,2560]{0,1:T(8,128)} %copy.15, f32[2560,1024]{1,0:T(8,128)} %fusion.14, bf16[1024,1024]{1,0:T(8,128)(2,1)} %all-gather.2.cloned.1.call-done, f32[2560,1024]{0,1:T(8,128)} %copy.16, f32[1024]{0:T(1024)S(1)} %get-tuple-element.16, s32[2560]{0:T(1024)S(1)} %iota_add_fusion, s32[1024]{0:T(1024)S(1)} %copy-done.1), kind=kOutput, calls=%fused_computation.11 | convolution fusion | flops 5394923520 | bytes 44058624 | tf_op jit(solution)/shard_map/dot_general | solution.py:50
  559.7 11.4 %copy.18 = f32[1024,2560]{1,0:T(8,128)} copy(f32[1024,2560]{0,1:T(8,128)} %fusion.6) | data formatting | bytes 20971520
  571.1 0.6 pad_maximum_fusion
  (9 shorter events, 0.0 us)
Async XLA Ops:
  31.3 7.9 %copy-start = (f32[256,1024]{1,0:T(8,128)S(1)}, f32[256,1024]{1,0:T(8,128)}, u32[]{:S(2)}) copy-start(f32[256,1024]{1,0:T(8,128)} %param.3) | copy-start | bytes 3145732
  31.3 243.4 %all-to-all-start = ((f32[32,32,20,128]{3,0,2,1:T(8,128)}), f32[32,32,20,128]{3,0,2,1:T(8,128)}, u32[]{:S(2)}, u32[]{:S(2)}) async-start(f32[32,32,20,128]{3,0,2,1:T(8,128)} %copy.13), calls=%async_computation | async-start | bytes 20971520 | tf_op jit(solution)/shard_map/all_to_all | solution.py:21
  38.8 287.0 %all-gather.2.cloned.1.call-start = ((), (), s32[]{:S(2)}) async-start(), calls=%async_computation.1 | async-start | bytes 2621440 | tf_op jit(solution)/shard_map/all_gather | solution.py:12
  325.8 48.2 %copy-start.1 = (s32[1024]{0:T(1024)S(1)}, s32[1024]{0:T(1024)}, u32[]{:S(2)}) copy-start(s32[1024]{0:T(1024)} %param.5) | copy-start | bytes 12292
  374.0 58.8 %slice-start = ((s8[10485760]{0:T(1024)(128)(4,1)}), s8[2097152]{0:T(1024)(128)(4,1)S(1)}, s32[]{:S(2)}) async-start(s8[10485760]{0:T(1024)(128)(4,1)} %bitcast.44), calls=%async_computation.2 | async-start | bytes 4194304
  420.7 12.0 %slice-start.1 = ((s8[10485760]{0:T(1024)(128)(4,1)}), s8[4194304]{0:T(1024)(128)(4,1)S(1)}, s32[]{:S(2)}) async-start(s8[10485760]{0:T(1024)(128)(4,1)} %bitcast.44), calls=%async_computation.3 | async-start | bytes 8388608
  420.7 12.0 %slice-start.2 = ((s8[10485760]{0:T(1024)(128)(4,1)}), s8[4194304]{0:T(1024)(128)(4,1)S(1)}, s32[]{:S(2)}) async-start(s8[10485760]{0:T(1024)(128)(4,1)} %bitcast.44), calls=%async_computation.4 | async-start | bytes 8388608
  420.7 12.0 %copy-start.2 = (bf16[1024,1024]{1,0:T(8,128)(2,1)S(1)}, bf16[1024,1024]{1,0:T(8,128)(2,1)}, u32[]{:S(2)}) copy-start(bf16[1024,1024]{1,0:T(8,128)(2,1)} %all-gather.2.cloned.1.call-done) | copy-start | bytes 6291460
Sparse Core Ops, SparseCore 0:
  41.1 74.9 all-gather.1
where the time goes:
time: 585 us; the launch traced here: 579 us
  waiting for transfers between devices  235 us (40%)
  blocking collectives  158 us (27%)
  local copies, waits for them, and re-layouts  98.1 us (17%)
  matrix products  52.9 us (9%)
  between operations  14.3 us (2%)
  other arithmetic  12.8 us (2%)
  starting transfers between devices  7.86 us (1%)
    all_to_all x1, waiting for transfers between devices, shards(): lax.all_to_all(pieces, ('cls', 'row'), split_axis=1, concat_axis=0, tiled...  235 us
    psum x2, blocking collectives, shards(): lax.psum((jnp.sum(jnp.exp(logits - row_peak[:, None]), axis=1), local_pic...  81.7 us
    pmax x2, blocking collectives, shards(): row_peak = lax.pmax(local_peak, ('cls', 'row'))  76.4 us
    unnamed x14, local copies, waits for them, and re-layouts  33.3 us
    dot_general x2, matrix products, shards(): lax.dot_general(examples, residual, (((0,), (0,)), ((), ())), preferred_e...  29.2 us
    reshape x2, local copies, waits for them, and re-layouts, shards(): pieces = weights.reshape(feature_rows, peer_count, class_count // 128, 128)  24.2 us
    all_to_all x1, local copies, waits for them, and re-layouts, shards(): lax.all_to_all(pieces, ('cls', 'row'), split_axis=1, concat_axis=0, tiled...  17.8 us
    dot_general x1, matrix products, shards(): jnp.dot(examples, current.astype(jnp.bfloat16), preferred_element_type=jn...  12.4 us
  transfers between devices with their start and end apart: 2, of which 1 were waited for; matrix products, arithmetic and copies ran while one was open for 9% of the time, Pallas kernels for 0%

commit v1 on v0

--- a/solution.py
+++ b/solution.py
@@ -5,6 +5,13 @@
 
 STEPS = 2
 learn_rate = 2.0
+
+
+def swap_blocks(x, axis, split, join):
+    peers = lax.axis_size(axis)
+    blocks = jnp.stack(jnp.split(x, peers, axis=split), axis=0)
+    blocks = lax.all_to_all(blocks, axis, split_axis=0, concat_axis=0)
+    return jnp.concatenate(blocks, axis=join)
 
 
 def shards(embeddings, weights, labels):
@@ -18,9 +25,7 @@
     columns = lax.broadcasted_iota(jnp.int32, (1, class_count), 1) + offset
     label_hit = columns == labels[:, None]
     pieces = weights.reshape(feature_rows, peer_count, class_count // 128, 128)
-    block_weights = lax.all_to_all(pieces, ("cls", "row"), split_axis=1, concat_axis=0, tiled=True)[
-        :, 0
-    ]
+    block_weights = swap_blocks(pieces, ("cls", "row"), 1, 0)[:, 0]
     block_width = block_weights.shape[1] * 128
     flat_weights = block_weights.reshape(block_weights.shape[0], block_width)
     block_logits = jnp.dot(

time: 585 us -> 613 us (1.048)
  local copies, waits for them, and re-layouts: 98.1 us -> 129 us
    unnamed x14 -> x45, local copies, waits for them, and re-layouts: 33.3 us -> 77.9 us
    reshape x2 -> x1, local copies, waits for them, and re-layouts: 24.2 us -> 9.43 us  [shards(): pieces = weights.reshape(feature_rows, peer_count, class_count // 128, 128)]
    another operation x0 -> x2, local copies, waits for them, and re-layouts: none -> 12.3 us  [swap_blocks(): blocks = jnp.stack(jnp.split(x, peers, axis=split), axis=0)]
    dot_general x1 -> x0, local copies, waits for them, and re-layouts: 11.5 us -> none  [shards(): jnp.dot(examples, current.astype(jnp.bfloat16), preferred_element_type=jn...]
  transfers between devices with their start and end apart: 2 -> 2, of which waited for: 1 -> 1; matrix products, arithmetic and copies ran while one was open for 9% -> 7% of each run, Pallas kernels for 0% -> 0%
where the time goes in v1:
time: 613 us; the launch traced here: 611 us
  waiting for transfers between devices  235 us (38%)
  blocking collectives  158 us (26%)
  local copies, waits for them, and re-layouts  129 us (21%)
  matrix products  54.1 us (9%)
  between operations  14.1 us (2%)
  other arithmetic  13.5 us (2%)
  starting transfers between devices  7.66 us (1%)
    all_to_all x1, waiting for transfers between devices, swap_blocks(): blocks = lax.all_to_all(blocks, axis, split_axis=0, concat_axis=0)  235 us
    psum x2, blocking collectives, shards(): lax.psum((jnp.sum(jnp.exp(logits - row_peak[:, None]), axis=1), local_pic...  81.7 us
    unnamed x45, local copies, waits for them, and re-layouts  77.9 us
    pmax x2, blocking collectives, shards(): row_peak = lax.pmax(local_peak, ('cls', 'row'))  76.4 us
    dot_general x2, matrix products, shards(): lax.dot_general(examples, residual, (((0,), (0,)), ((), ())), preferred_e...  30.4 us
    all_to_all x1, local copies, waits for them, and re-layouts, swap_blocks(): blocks = lax.all_to_all(blocks, axis, split_axis=0, concat_axis=0)  17.8 us
    dot_general x1, matrix products, shards(): jnp.dot(examples, current.astype(jnp.bfloat16), preferred_element_type=jn...  12.3 us
    another operation x2, local copies, waits for them, and re-layouts, swap_blocks(): blocks = jnp.stack(jnp.split(x, peers, axis=split), axis=0)  12.3 us
  transfers between devices with their start and end apart: 2, of which 1 were waited for; matrix products, arithmetic and copies ran while one was open for 7% of the time, Pallas kernels for 0%

profile of v1, /device:TPU:0, one launch (start us, length us, event | category | flops | bytes accessed | tf_op | source)
XLA Modules:
  0.0 611.1 jit_solution(14898318579559688674)
XLA Ops:
  7.2 9.4 %reshape.17 = f32[32,32,20,128]{3,2,1,0:T(8,128)} reshape(f32[32,81920]{1,0:T(8,128)} %param.4) | data formatting | bytes 20971520 | tf_op jit(solution)/shard_map/reshape | solution.py:27
  16.6 1.8 fusion.63
  18.4 1.8 fusion.62
  20.2 1.8 fusion.61
  29.1 1.8 fusion.56
  30.9 1.8 fusion.55
  32.6 1.8 fusion.54
  34.4 1.8 fusion.53
  38.0 1.8 fusion.51
  39.8 1.8 fusion.50
  41.6 1.8 fusion.49
  55.8 1.8 fusion.41
  57.5 1.8 fusion.40
  61.1 1.8 fusion.38
  71.7 1.8 fusion.32
  73.5 10.5 %copy.103 = f32[32,32,1,20,128]{4,1,3,2,0:T(8,128)} copy(f32[32,32,1,20,128]{4,3,1,2,0:T(8,128)} %fusion.32) | data formatting | bytes 20971520 | tf_op jit(solution)/shard_map/stack | solution.py:12
  84.0 7.4 %all-to-all-start = ((f32[32,32,1,20,128]{4,1,3,2,0:T(8,128)}), f32[32,32,1,20,128]{4,1,3,2,0:T(8,128)}, u32[]{:S(2)}, u32[]{:S(2)}) async-start(f32[32,32,1,20,128]{4,1,3,2,0:T(8,128)} %copy.103), calls=%async_computation | async-start | bytes 20971520 | tf_op jit(solution)/shard_map/all_to_all | solution.py:13
  92.7 234.7 %all-to-all-done = f32[32,32,1,20,128]{4,1,3,2,0:T(8,128)} async-done(((f32[32,32,1,20,128]{4,1,3,2,0:T(8,128)}), f32[32,32,1,20,128]{4,1,3,2,0:T(8,128)}, u32[]{:S(2)}, u32[]{:S(2)}) %all-to-all-start) | async-done | bytes 10485792 | tf_op jit(solution)/shard_map/all_to_all | solution.py:13
  327.4 17.8 %copy.104 = f32[32,32,1,20,128]{4,3,1,0,2:T(8,128)} copy(f32[32,32,1,20,128]{4,1,3,2,0:T(8,128)} %all-to-all-done) | data formatting | bytes 20971520 | tf_op jit(solution)/shard_map/all_to_all | solution.py:13
  345.2 11.4 %copy.141 = f32[128,8,20,128]{3,1,2,0:T(8,128)} copy(f32[128,8,20,128]{3,2,1,0:T(8,128)} %bitcast.241) | data formatting | bytes 20971520
  356.6 11.4 %copy.105 = f32[1024,2560]{0,1:T(8,128)} copy(f32[1024,2560]{1,0:T(8,128)} %bitcast.242) | data formatting | bytes 20971520 | tf_op jit(solution)/shard_map/reshape;squeeze;reshape | solution.py:35
  368.0 11.3 %fusion.70 = (f32[1024]{0:T(1024)S(1)}, f32[2560,1024]{1,0:T(8,128)}) fusion(bf16[1024,1024]{1,0:T(8,128)(2,1)} %all-gather.2.cloned.1.call-done, f32[1024,2560]{1,0:T(8,128)} %bitcast.243), kind=kOutput, calls=%fused_computation.113 | convolution fusion | flops 5373950976 | bytes 23072768 | tf_op jit(solution)/shard_map/dot_general | solution.py:31
  379.3 36.8 %pmax.14 = f32[1024]{0:T(1024)S(1)} all-reduce(f32[1024]{0:T(1024)S(1)} %get-tuple-element.17), channel_id=1, replica_groups=mesh['cls'=8,'row'=4] {'cls','row'}, use_global_device_ids=true, to_apply=%region_1.2 | all-reduce | flops 1024 | bytes 8192 | tf_op jit(solution)/shard_map/pmax | solution.py:46
  416.1 6.0 fusion.4
  422.2 41.0 %psum.28 = f32[1024]{0:T(1024)S(1)} all-reduce(f32[1024]{0:T(1024)S(1)} %get-tuple-element.9), channel_id=1, replica_groups=mesh['cls'=8,'row'=4] {'cls','row'}, use_global_device_ids=true, to_apply=%region_3.4 | all-reduce | flops 1024 | bytes 8192 | tf_op jit(solution)/shard_map/psum | solution.py:47
  463.2 12.0 %fusion.17 = f32[2560,1024]{1,0:T(8,128)} fusion(bf16[1024,1024]{1,0:T(8,128)(2,1)} %all-gather.2.cloned.1.call-done, f32[2560,1024]{1,0:T(8,128)} %get-tuple-element.18, s32[1024]{0:T(1024)S(1)} %copy-done.1, f32[1024]{0:T(1024)S(1)} %log_add_fusion.1, s32[2560]{0:T(1024)S(1)} %iota_add_fusion), kind=kOutput, calls=%fused_computation.25 | convolution fusion | flops 5381816320 | bytes 23087104 | tf_op jit(solution)/shard_map/dot_general | solution.py:55
  475.2 12.3 %fusion.71 = (f32[1024]{0:T(1024)S(1)}, f32[2560,1024]{1,0:T(8,128)}) fusion(bf16[1024,1024]{1,0:T(8,128)(2,1)S(1)} %copy-done.2, f32[1024,2560]{0,1:T(8,128)S(1)} %bitcast.245, f32[2560,1024]{1,0:T(8,128)} %fusion.17), kind=kOutput, calls=%fused_computation.114 | convolution fusion | flops 5379193856 | bytes 33558528 | tf_op jit(solution)/shard_map/dot_general | solution.py:41
  487.6 39.6 %pmax.15 = f32[1024]{0:T(1024)S(1)} all-reduce(f32[1024]{0:T(1024)S(1)} %get-tuple-element.19), channel_id=1, replica_groups=mesh['cls'=8,'row'=4] {'cls','row'}, use_global_device_ids=true, to_apply=%region_5.6 | all-reduce | flops 1024 | bytes 8192 | tf_op jit(solution)/shard_map/pmax | solution.py:46
  527.2 5.9 fusion.5
  533.1 40.7 %all-reduce = (f32[1024]{0:T(1024)S(1)}, f32[1024]{0:T(1024)S(1)}, f32[1024]{0:T(1024)S(1)}) all-reduce(f32[1024]{0:T(1024)S(1)} %get-tuple-element.11, f32[1024]{0:T(1024)S(1)} %get-tuple-element.10, f32[1024]{0:T(1024)S(1)} %get-tuple-element.8), channel_id=1, replica_groups=mesh['cls'=8,'row'=4] {'cls','row'}, use_global_device_ids=true, to_apply=%region_7.8 | all-reduce | flops 3072 | bytes 24576 | tf_op jit(solution)/shard_map/psum | solution.py:47
  573.8 18.4 %fusion.6 = f32[1024,2560]{0,1:T(8,128)} fusion(f32[1024,2560]{0,1:T(8,128)} %copy.105, f32[2560,1024]{1,0:T(8,128)} %fusion.17, bf16[1024,1024]{1,0:T(8,128)(2,1)} %all-gather.2.cloned.1.call-done, f32[2560,1024]{1,0:T(8,128)} %get-tuple-element.20, f32[1024]{0:T(1024)S(1)} %get-tuple-element.16, s32[1024]{0:T(1024)S(1)} %copy-done.1, ...), kind=kOutput, calls=%fused_computation.11 | convolution fusion | flops 5394923520 | bytes 44058624 | tf_op jit(solution)/shard_map/dot_general | solution.py:55
  592.3 11.4 %copy.107 = f32[1024,2560]{1,0:T(8,128)} copy(f32[1024,2560]{0,1:T(8,128)} %fusion.6) | data formatting | bytes 20971520
  (40 shorter events, 33.7 us)
Async XLA Ops:
  84.0 7.7 %copy-start = (f32[256,1024]{1,0:T(8,128)S(1)}, f32[256,1024]{1,0:T(8,128)}, u32[]{:S(2)}) copy-start(f32[256,1024]{1,0:T(8,128)} %param.3) | copy-start | bytes 3145732
  84.0 243.4 %all-to-all-start = ((f32[32,32,1,20,128]{4,1,3,2,0:T(8,128)}), f32[32,32,1,20,128]{4,1,3,2,0:T(8,128)}, u32[]{:S(2)}, u32[]{:S(2)}) async-start(f32[32,32,1,20,128]{4,1,3,2,0:T(8,128)} %copy.103), calls=%async_computation | async-start | bytes 20971520 | tf_op jit(solution)/shard_map/all_to_all | solution.py:13
  91.5 276.5 %all-gather.2.cloned.1.call-start = ((), (), s32[]{:S(2)}) async-start(), calls=%async_computation.1 | async-start | bytes 2621440 | tf_op jit(solution)/shard_map/all_gather | solution.py:19
  368.0 48.1 %copy-start.1 = (s32[1024]{0:T(1024)S(1)}, s32[1024]{0:T(1024)}, u32[]{:S(2)}) copy-start(s32[1024]{0:T(1024)} %param.5) | copy-start | bytes 12292
  416.1 59.1 %slice-start = ((s8[10485760]{0:T(1024)(128)(4,1)}), s8[2097152]{0:T(1024)(128)(4,1)S(1)}, s32[]{:S(2)}) async-start(s8[10485760]{0:T(1024)(128)(4,1)} %bitcast.244), calls=%async_computation.2 | async-start | bytes 4194304
  463.2 12.0 %slice-start.1 = ((s8[10485760]{0:T(1024)(128)(4,1)}), s8[4194304]{0:T(1024)(128)(4,1)S(1)}, s32[]{:S(2)}) async-start(s8[10485760]{0:T(1024)(128)(4,1)} %bitcast.244), calls=%async_computation.3 | async-start | bytes 8388608
  463.2 12.0 %slice-start.2 = ((s8[10485760]{0:T(1024)(128)(4,1)}), s8[4194304]{0:T(1024)(128)(4,1)S(1)}, s32[]{:S(2)}) async-start(s8[10485760]{0:T(1024)(128)(4,1)} %bitcast.244), calls=%async_computation.4 | async-start | bytes 8388608
  463.2 12.0 %copy-start.2 = (bf16[1024,1024]{1,0:T(8,128)(2,1)S(1)}, bf16[1024,1024]{1,0:T(8,128)(2,1)}, u32[]{:S(2)}) copy-start(bf16[1024,1024]{1,0:T(8,128)(2,1)} %all-gather.2.cloned.1.call-done) | copy-start | bytes 6291460
Sparse Core Ops, SparseCore 0:
  93.9 74.9 all-gather.1
